TPU v7x, 32 devices: a whole 2x2x4 slice. The times are simulated.
32 devices in a mesh: gx: 4 (over y, x), gy: 2 (over core), gz: 4 (over z).
Axes of the slice: x: 2, y: 2, z: 4, core: 2. Of those that a mesh axis runs over, the one named last changes fastest.
Arguments:
- labels: int32 [128, 128, 512], P('gx', 'gy', 'gz'), may hold values from 0 to 7
- conductivity: float32 [7, 8], replicated, may hold values from -0.08 to 2, as said below
- right_side: float32 [128, 128, 512], P('gx', 'gy', 'gz'), may hold values from -18 to 18
Outputs:
- solution: float32 [128, 128, 512], P('gx', 'gy', 'gz')
Inputs may be any that keep to these rules, and one draw needn't show every extreme that they name: `conductivity`: rows 0 to 2 are positive, rows 3 to 5 have magnitude at most 0.08, row 6 is at least 0.5.
All inputs are finite; a program needn't handle non-finite values.
Results may differ from a plain program's by a relative error of at most 0.0001.
Values sent between devices are 32-bit elements; how exact they have to be, the bound alone decides.
A program may use at most 128 MiB of HBM per device.

v0:
```python
import jax
import jax.numpy as jnp
from jax import lax
from jax.sharding import PartitionSpec as P

ITERS = 3


def with_halo(cells, sides, width):
    for axis, dim in sides:
        count = lax.axis_size(axis)
        ends = count - 1
        head = lax.slice_in_dim(cells, 0, width, axis=dim)
        tail = lax.slice_in_dim(cells, cells.shape[dim] - width, cells.shape[dim], axis=dim)
        cells = jnp.concatenate(
            [
                lax.ppermute(tail, axis, [(i, (i + 1) % count) for i in range(ends)]),
                cells,
                lax.ppermute(head, axis, [((i + 1) % count, i) for i in range(ends)]),
            ],
            axis=dim,
        )
    return cells


def neighbour_value(arr, shift_x, shift_y, shift_z, cell_grid):
    size_x, size_y, size_z = cell_grid
    return arr[
        ...,
        1 + shift_x : 1 + shift_x + size_x,
        1 + shift_y : 1 + shift_y + size_y,
        1 + shift_z : 1 + shift_z + size_z,
    ]


def stencil_apply(padded_value, padded_sigma, self_coefficient):
    cell_grid = self_coefficient.shape
    value_entry = neighbour_value(padded_value, 0, 0, 0, cell_grid)
    total_flux = self_coefficient * value_entry
    for axis in range(3):
        for sign in (-1, 1):
            stencil_offset = [0, 0, 0]
            stencil_offset[axis] = sign
            face_flux = 0.5 * (
                neighbour_value(padded_sigma[axis], 0, 0, 0, cell_grid)
                + neighbour_value(
                    padded_sigma[axis],
                    stencil_offset[0],
                    stencil_offset[1],
                    stencil_offset[2],
                    cell_grid,
                )
            )
            total_flux = total_flux + face_flux * (
                value_entry
                - neighbour_value(
                    padded_value, stencil_offset[0], stencil_offset[1], stencil_offset[2], cell_grid
                )
            )
    for first, second, comp in ((0, 1, 3), (0, 2, 4), (1, 2, 5)):
        for sign_a in (-1, 1):
            for sign_b in (-1, 1):
                stencil_offset = [0, 0, 0]
                stencil_offset[first] = sign_a
                stencil_offset[second] = sign_b
                cross_term = (
                    0.25
                    * sign_a
                    * sign_b
                    * (
                        neighbour_value(padded_sigma[comp], 0, 0, 0, cell_grid)
                        + neighbour_value(
                            padded_sigma[comp],
                            stencil_offset[0],
                            stencil_offset[1],
                            stencil_offset[2],
                            cell_grid,
                        )
                    )
                )
                total_flux = total_flux - cross_term * neighbour_value(
                    padded_value, stencil_offset[0], stencil_offset[1], stencil_offset[2], cell_grid
                )
    return total_flux


def diagonal_of(padded_sigma, self_coefficient):
    cell_grid = self_coefficient.shape
    total_flux = self_coefficient
    for axis in range(3):
        for sign in (-1, 1):
            stencil_offset = [0, 0, 0]
            stencil_offset[axis] = sign
            total_flux = total_flux + 0.5 * (
                neighbour_value(padded_sigma[axis], 0, 0, 0, cell_grid)
                + neighbour_value(
                    padded_sigma[axis],
                    stencil_offset[0],
                    stencil_offset[1],
                    stencil_offset[2],
                    cell_grid,
                )
            )
    return total_flux


def lookup(shifted, conductivity):
    total_flux = jnp.zeros((7,) + shifted.shape, jnp.float32)
    for label in range(conductivity.shape[1]):
        hit = (shifted == label + 1).astype(jnp.float32)
        total_flux = total_flux + hit[None] * conductivity[:, label][:, None, None, None]
    return total_flux


def apply_operator(field, padded_sigma, self_coefficient):
    field_pad = with_halo(field, (("gx", 0), ("gy", 1), ("gz", 2)), 1)
    return stencil_apply(field_pad, padded_sigma, self_coefficient)


def local(labels, conductivity, right_side):
    shifted = labels + 1
    own_table = lookup(shifted, conductivity)
    padded_sigma = with_halo(own_table[:6], (("gx", 1), ("gy", 2), ("gz", 3)), 1)
    self_coefficient = own_table[6]
    diag = diagonal_of(padded_sigma, self_coefficient)
    solution = jnp.zeros_like(right_side)
    residual = right_side
    precond = residual / diag
    applied = apply_operator(precond, padded_sigma, self_coefficient)
    gamma_old = jnp.float32(1.0)
    alpha_old = jnp.float32(1.0)
    direction = precond
    for step in range(ITERS):
        gamma, delta = lax.psum(
            (jnp.sum(residual * precond), jnp.sum(applied * precond)), ("gx", "gy", "gz")
        )
        if step + 1 < ITERS:
            scaled = applied / diag
            product = apply_operator(scaled, padded_sigma, self_coefficient)
        if step == 0:
            alpha = gamma / delta
            direction = precond
            along_z = product
            along_q = scaled
            along_s = applied
        else:
            ratio = gamma / gamma_old
            alpha = gamma / (delta - ratio * gamma / alpha_old)
            direction = precond + ratio * direction
            if step + 1 < ITERS:
                along_z = product + ratio * along_z
                along_q = scaled + ratio * along_q
                along_s = applied + ratio * along_s
        solution = solution + alpha * direction
        if step + 1 < ITERS:
            residual = residual - alpha * along_s
            precond = precond - alpha * along_q
            applied = applied - alpha * along_z
        gamma_old = gamma
        alpha_old = alpha
    return solution


def solution(mesh):
    return jax.shard_map(
        local,
        mesh=mesh,
        in_specs=(P("gx", "gy", "gz"), P(), P("gx", "gy", "gz")),
        out_specs=P("gx", "gy", "gz"),
        check_vma=False,
    )
```

profile of v0, /device:TPU:0, one launch (start us, length us, event | category | flops | bytes accessed | tf_op | source)
XLA Modules:
  0.0 398.3 jit_solution(9120328655755178801)
XLA Ops:
  1.3 2.3 compare_convert_fusion.7
  3.6 4.1 %multiply_add_fusion = f32[7,32,64,128]{3,2,1,0:T(8,128)S(1)} fusion(f32[7]{0:T(128)S(1)} %get-tuple-element.15, f32[32,64,128]{2,1,0:T(8,128)S(1)} %get-tuple-element.83, f32[7]{0:T(128)S(1)} %get-tuple-element.16, f32[32,64,128]{2,1,0:T(8,128)S(1)} %get-tuple-element.82, f32[7]{0:T(128)S(1)} %get-tuple-element.10, f32[32,64,128]{2,1,0:T(8,128)S(1)} %get-tuple-element.81, ...), kind=kLoop, calls=%fused_computation.2 | loop fusion | flops 27525120 | bytes 15728864 | tf_op jit(solution)/shard_map/add | solution.py:111
  7.8 4.9 %collective-permute-start = (f32[6,1,64,128]{3,2,1,0:T(8,128)S(1)}, f32[6,1,64,128]{3,2,1,0:T(8,128)S(1)}, u32[]{:S(2)}, u32[]{:S(2)}) collective-permute-start(f32[6,1,64,128]{3,2,1,0:T(8,128)S(1)} %get-tuple-element.42), channel_id=1, source_target_pairs={{0,8},{8,16},{16,24},{1,9},{9,17},{17,25},{2,10},{10,18},{18,26},{... | collective-permute-start | bytes 589832 | tf_op jit(solution)/shard_map/ppermute | solution.py:17
  16.8 6.2 %collective-permute-done.1 = f32[6,1,64,128]{3,2,1,0:T(8,128)S(1)} collective-permute-done((f32[6,1,64,128]{3,2,1,0:T(8,128)S(1)}, f32[6,1,64,128]{3,2,1,0:T(8,128)S(1)}, u32[]{:S(2)}, u32[]{:S(2)}) %collective-permute-start.1) | collective-permute-done | bytes 196640 | tf_op jit(solution)/shard_map/ppermute | solution.py:19
  27.6 3.6 pad_maximum_fusion.1
  31.2 12.6 %fusion.111 = (f32[6,34,66,1]{3,2,1,0:T(8,128)}, f32[6,34,66,1]{3,2,1,0:T(8,128)}) fusion(f32[6,34,66,128]{3,2,1,0:T(8,128)} %pad_maximum_fusion.1), kind=kLoop, calls=%fused_computation.239 | loop fusion | bytes 215424 | tf_op jit(solution)/shard_map/slice | solution.py:14
  43.8 5.1 %copy.16 = f32[6,34,66,1]{2,3,1,0:T(1,128)S(1)} copy(f32[6,34,66,1]{3,2,1,0:T(8,128)} %get-tuple-element.40) | data formatting | bytes 107712 | tf_op jit(solution)/shard_map/slice | solution.py:14
  48.9 3.5 collective-permute-start.4
  52.4 5.1 %copy.17 = f32[6,34,66,1]{2,3,1,0:T(1,128)S(1)} copy(f32[6,34,66,1]{3,2,1,0:T(8,128)} %get-tuple-element.41) | data formatting | bytes 107712 | tf_op jit(solution)/shard_map/slice | solution.py:13
  59.0 4.9 %copy.18 = f32[6,34,66,1]{3,2,1,0:T(8,128)} copy(f32[6,34,66,1]{2,3,1,0:T(1,128)S(1)} %collective-permute-done.4) | data formatting | bytes 107712 | tf_op jit(solution)/shard_map/ppermute | solution.py:17
  64.1 4.7 %copy.19 = f32[6,34,66,1]{3,2,1,0:T(8,128)} copy(f32[6,34,66,1]{2,3,1,0:T(1,128)S(1)} %collective-permute-done.5) | data formatting | bytes 107712 | tf_op jit(solution)/shard_map/ppermute | solution.py:19
  68.7 18.9 %pad_maximum_fusion = f32[6,34,66,130]{3,2,1,0:T(8,128)} fusion(f32[6,34,66,1]{3,2,1,0:T(8,128)} %copy.19, f32[6,34,1,128]{3,2,1,0:T(1,128)S(1)} %collective-permute-done.3, f32[6,1,64,128]{3,2,1,0:T(8,128)S(1)} %collective-permute-done.1, f32[6,32,64,128]{3,2,1,0:T(8,128)} %copy-done.9, f32[6,1,64,128]{3,2,1,0:T(8,128)S(1)} %collective-permute-done, ...), kind=kLoop, calls=%fused_computation | loop fusion | flops 10501920 | bytes 14002560 | tf_op jit(solution)/shard_map/concatenate | solution.py:15
  87.6 10.2 %slice_bitcast_fusion.2 = (f32[34,66,130]{2,1,0:T(8,128)S(1)}, f32[34,66,130]{2,1,0:T(8,128)}, f32[34,66,130]{2,1,0:T(8,128)}, f32[34,66,130]{2,1,0:T(8,128)}, f...) fusion(f32[6,34,66,130]{3,2,1,0:T(8,128)} %pad_maximum_fusion), kind=kLoop, calls=%fused_computation.5 | loop fusion | bytes 14002560 | tf_op jit(solution)/shard_map/squeeze | solution.py:71
  97.8 13.2 %fusion.104 = (f32[32,64,128]{2,1,0:T(8,128)S(1)}, f32[32,64,128]{2,1,0:T(8,128)}, f32[32,64,128]{2,1,0:T(8,128)}, f32[32,64,128]{2,1,0:T(8,128)}, f32[32,64,128...) fusion(f32[32,64,128]{2,1,0:T(8,128)} %param.5, ...), kind=kLoop, calls=%fused_computation.238 | loop fusion | flops 4980736 | bytes 19922944 | tf_op jit(solution)/shard_map/div | solution.py:128
  111.0 3.4 collective-permute-start.6
  116.0 4.2 %collective-permute-done.7 = f32[1,64,128]{2,1,0:T(8,128)S(1)} collective-permute-done((f32[1,64,128]{2,1,0:T(8,128)S(1)}, f32[1,64,128]{2,1,0:T(8,128)S(1)}, u32[]{:S(2)}, u32[]{:S(2)}) %collective-permute-start.7) | collective-permute-done | bytes 32800 | tf_op jit(solution)/shard_map/ppermute | solution.py:19
  127.2 2.4 copy.20
  129.6 2.4 copy.22
  133.3 5.6 %collective-permute-start.10 = (f32[34,66,1]{1,2,0:T(1,128)}, f32[34,66,1]{1,2,0:T(1,128)}, u32[]{:S(2)}, u32[]{:S(2)}) collective-permute-start(f32[34,66,1]{1,2,0:T(1,128)} %copy.20), channel_id=1, source_target_pairs={{0,1},{1,2},{2,3},{4,5},{5,6},{6,7},{8,9},{9,10},{10,11},{12,13},{... | collective-permute-start | bytes 26936 | tf_op jit(solution)/shard_map/ppermute | solution.py:17
  138.8 2.5 maximum_maximum_fusion.3
  141.3 2.3 copy.21
  143.6 2.4 copy.23
  146.0 3.8 maximum_maximum_fusion
  150.2 9.8 %multiply_reduce_fusion.3 = (f32[]{:T(128)}, f32[]{:T(128)}, f32[32,64,128]{2,1,0:T(8,128)S(1)}) fusion(f32[32,64,128]{2,1,0:T(8,128)S(1)} %get-tuple-element.26, f32[32,64,128]{2,1,0:T(8,128)} %param.5, f32[34,66,129]{2,1,0:T(8,128)S(1)} %get-tuple-element.57, f32[34,66,130]{2,1,0:T(8,128)S(1)} %copy-done, f32[34,66,129]{2,1,0:T(8,128)S(1)} %get-tuple-element.56, ...), kind=kLoop, calls=%fused_computation.206 | loop fusion | flops 19136512 | bytes 43057160 | tf_op jit(solution)/shard_map/reduce_sum | solution.py:135
  160.2 2.8 collective-permute-start.12
  164.6 4.2 %collective-permute-done.13 = f32[1,64,128]{2,1,0:T(8,128)S(1)} collective-permute-done((f32[1,64,128]{2,1,0:T(8,128)S(1)}, f32[1,64,128]{2,1,0:T(8,128)S(1)}, u32[]{:S(2)}, u32[]{:S(2)}) %collective-permute-start.13) | collective-permute-done | bytes 32800 | tf_op jit(solution)/shard_map/ppermute | solution.py:19
  172.6 40.9 %all-reduce.2 = (f32[]{:T(128)}, f32[]{:T(128)}) all-reduce(f32[]{:T(128)} %get-tuple-element.8, f32[]{:T(128)} %get-tuple-element.7), channel_id=1, replica_groups=mesh['gx'=4,'gy'=2,'gz'=4] {'gx','gy','gz'}, use_global_device_ids=true, to_apply=%region_1.0 | all-reduce | flops 2 | bytes 16 | tf_op jit(solution)/shard_map/psum | solution.py:134
  218.1 2.4 copy.24
  220.5 2.4 copy.26
  224.1 5.1 %collective-permute-start.16 = (f32[34,66,1]{1,2,0:T(1,128)}, f32[34,66,1]{1,2,0:T(1,128)}, u32[]{:S(2)}, u32[]{:S(2)}) collective-permute-start(f32[34,66,1]{1,2,0:T(1,128)} %copy.24), channel_id=1, source_target_pairs={{0,1},{1,2},{2,3},{4,5},{5,6},{6,7},{8,9},{9,10},{10,11},{12,13},{... | collective-permute-start | bytes 26936 | tf_op jit(solution)/shard_map/ppermute | solution.py:17
  229.3 3.3 maximum_maximum_fusion.4
  232.6 2.3 copy.25
  234.8 2.4 copy.27
  237.2 4.1 %maximum_maximum_fusion.1 = (f32[34,66,129]{2,1,0:T(8,128)S(1)}, f32[34,66,129]{2,1,0:T(8,128)S(1)}) fusion(f32[34,1,128]{2,1,0:T(1,128)} %collective-permute-done.15, f32[1,64,128]{2,1,0:T(8,128)} %copy-done.26, f32[32,64,128]{2,1,0:T(8,128)} %copy-done.6, f32[1,64,128]{2,1,0:T(8,128)} %copy-done.24, f32[34,1,128]{2,1,0:T(1,128)} %collective-permute-done.14, ...), kind=kLoop, calls=%fused_computation.11 | loop fusion | flops 2894760 | bytes 3482688 | tf_op jit(solution)/shard_map/concatenate | solution.py:15
  242.0 9.4 %fusion.101 = (f32[32,64,128]{2,1,0:T(8,128)S(1)}, f32[32,64,128]{2,1,0:T(8,128)S(1)}) fusion(f32[32,64,128]{2,1,0:T(8,128)S(1)} %copy-done.18, f32[32,64,128]{2,1,0:T(8,128)S(1)} %copy-done.11, f32[]{:T(128)S(6)} %div.31, f32[34,66,129]{2,1,0:T(8,128)S(1)} %get-tuple-element.55, f32[34,66,130]{2,1,0:T(8,128)S(1)} %copy-done.1, ...), kind=kLoop, calls=%fused_computation.217 | loop fusion | flops 18874368 | bytes 45154308 | tf_op jit(solution)/shard_map/div | solution.py:138
  252.2 4.8 %collective-permute-start.18 = (f32[1,64,128]{2,1,0:T(8,128)}, f32[1,64,128]{2,1,0:T(8,128)}, u32[]{:S(2)}, u32[]{:S(2)}) collective-permute-start(f32[1,64,128]{2,1,0:T(8,128)} %get-tuple-element.70), channel_id=1, source_target_pairs={{0,8},{8,16},{16,24},{1,9},{9,17},{17,25},{2,10},{10,18},{18,26},{... | collective-permute-start | bytes 98312 | tf_op jit(solution)/shard_map/ppermute | solution.py:17
  259.5 41.2 %all-reduce.1 = (f32[]{:T(128)}, f32[]{:T(128)}) all-reduce(f32[]{:T(128)} %get-tuple-element.6, f32[]{:T(128)} %get-tuple-element.5), channel_id=1, replica_groups=mesh['gx'=4,'gy'=2,'gz'=4] {'gx','gy','gz'}, use_global_device_ids=true, to_apply=%region_5.0 | all-reduce | flops 2 | bytes 16 | tf_op jit(solution)/shard_map/psum | solution.py:134
  309.1 3.8 multiply_reduce_fusion
  315.7 2.4 copy.28
  318.0 2.4 copy.30
  321.7 5.1 %collective-permute-start.22 = (f32[34,66,1]{1,2,0:T(1,128)}, f32[34,66,1]{1,2,0:T(1,128)}, u32[]{:S(2)}, u32[]{:S(2)}) collective-permute-start(f32[34,66,1]{1,2,0:T(1,128)} %copy.28), channel_id=1, source_target_pairs={{0,1},{1,2},{2,3},{4,5},{5,6},{6,7},{8,9},{9,10},{10,11},{12,13},{... | collective-permute-start | bytes 26936 | tf_op jit(solution)/shard_map/ppermute | solution.py:17
  326.8 3.3 maximum_maximum_fusion.5
  330.1 2.3 copy.29
  332.4 2.4 copy.31
  334.8 4.1 %maximum_maximum_fusion.2 = (f32[34,66,129]{2,1,0:T(8,128)S(1)}, f32[34,66,129]{2,1,0:T(8,128)S(1)}) fusion(f32[34,1,128]{2,1,0:T(1,128)} %copy-done.34, f32[1,64,128]{2,1,0:T(8,128)} %collective-permute-done.19, f32[32,64,128]{2,1,0:T(8,128)} %copy-done.14, f32[1,64,128]{2,1,0:T(8,128)} %collective-permute-done.18, f32[34,1,128]{2,1,0:T(1,128)} %copy-done.32, ...), kind=kLoop, calls=%fused_computation.13 | loop fusion | flops 2894760 | bytes 3482688 | tf_op jit(solution)/shard_map/concatenate | solution.py:15
  339.6 10.8 %fusion.5 = f32[]{:T(128)} fusion(f32[34,66,129]{2,1,0:T(8,128)S(1)} %get-tuple-element.53, f32[34,66,129]{2,1,0:T(8,128)S(1)} %get-tuple-element.52, f32[34,65,128]{2,1,0:T(8,128)} %get-tuple-element.59, f32[34,65,128]{2,1,0:T(8,128)} %get-tuple-element.58, f32[32,64,128]{2,1,0:T(8,128)} %get-tuple-element.33, f32[32,64,128]{2,1,0:T(8,128)S(1)} %copy-done.16, ...), kind=kLoop, calls=%fused_computation.30 | loop fusion | flops 22020096 | bytes 46202896 | tf_op jit(solution)/shard_map/reduce_sum | solution.py:135
  350.3 40.4 %all-reduce = (f32[]{:T(128)}, f32[]{:T(128)}) all-reduce(f32[]{:T(128)} %multiply_reduce_fusion, f32[]{:T(128)} %fusion.5), channel_id=1, replica_groups=mesh['gx'=4,'gy'=2,'gz'=4] {'gx','gy','gz'}, use_global_device_ids=true, to_apply=%region_9.0 | all-reduce | flops 2 | bytes 16 | tf_op jit(solution)/shard_map/psum | solution.py:134
  394.5 3.8 multiply_add_fusion.1
  (127 shorter events, 44.8 us)
Async XLA Ops:
  7.7 7.4 %copy-start.13 = (f32[7,32,64,128]{3,2,1,0:T(8,128)}, f32[7,32,64,128]{3,2,1,0:T(8,128)S(1)}, u32[]{:S(2)}) copy-start(f32[7,32,64,128]{3,2,1,0:T(8,128)S(1)} %multiply_add_fusion) | copy-start | bytes 22020100
  7.8 9.0 %collective-permute-start = (f32[6,1,64,128]{3,2,1,0:T(8,128)S(1)}, f32[6,1,64,128]{3,2,1,0:T(8,128)S(1)}, u32[]{:S(2)}, u32[]{:S(2)}) collective-permute-start(f32[6,1,64,128]{3,2,1,0:T(8,128)S(1)} %get-tuple-element.42), channel_id=1, source_target_pairs={{0,8},{8,16},{16,24},{1,9},{9,17},{17,25},{2,10},{10,18},{18,26},{... | collective-permute-start | bytes 589832 | tf_op jit(solution)/shard_map/ppermute | solution.py:17
  12.7 10.3 %collective-permute-start.1 = (f32[6,1,64,128]{3,2,1,0:T(8,128)S(1)}, f32[6,1,64,128]{3,2,1,0:T(8,128)S(1)}, u32[]{:S(2)}, u32[]{:S(2)}) collective-permute-start(f32[6,1,64,128]{3,2,1,0:T(8,128)S(1)} %get-tuple-element.43), channel_id=1, source_target_pairs={{8,0},{16,8},{24,16},{9,1},{17,9},{25,17},{10,2},{18,10},{26,18},{... | collective-permute-start | bytes 589832 | tf_op jit(solution)/shard_map/ppermute | solution.py:19
  15.1 12.5 %copy-start.9 = (f32[6,32,64,128]{3,2,1,0:T(8,128)}, f32[6,32,64,128]{3,2,1,0:T(8,128)S(1)}, u32[]{:S(2)}) copy-start(f32[6,32,64,128]{3,2,1,0:T(8,128)S(1)} %slice.740) | copy-start | bytes 18874372
  23.1 2.6 collective-permute-start.2
  24.4 3.2 collective-permute-start.3
  48.9 10.1 %collective-permute-start.4 = (f32[6,34,66,1]{2,3,1,0:T(1,128)S(1)}, f32[6,34,66,1]{2,3,1,0:T(1,128)S(1)}, u32[]{:S(2)}, u32[]{:S(2)}) collective-permute-start(f32[6,34,66,1]{2,3,1,0:T(1,128)S(1)} %copy.16), channel_id=1, source_target_pairs={{0,1},{1,2},{2,3},{4,5},{5,6},{6,7},{8,9},{9,10},{10,11},{12,13},{... | collective-permute-start | bytes 161576 | tf_op jit(solution)/shard_map/ppermute | solution.py:17
  57.5 6.6 %collective-permute-start.5 = (f32[6,34,66,1]{2,3,1,0:T(1,128)S(1)}, f32[6,34,66,1]{2,3,1,0:T(1,128)S(1)}, u32[]{:S(2)}, u32[]{:S(2)}) collective-permute-start(f32[6,34,66,1]{2,3,1,0:T(1,128)S(1)} %copy.17), channel_id=1, source_target_pairs={{1,0},{2,1},{3,2},{5,4},{6,5},{7,6},{9,8},{10,9},{11,10},{13,12},{... | collective-permute-start | bytes 161576 | tf_op jit(solution)/shard_map/ppermute | solution.py:19
  111.0 5.0 %collective-permute-start.6 = (f32[1,64,128]{2,1,0:T(8,128)S(1)}, f32[1,64,128]{2,1,0:T(8,128)S(1)}, u32[]{:S(2)}, u32[]{:S(2)}) collective-permute-start(f32[1,64,128]{2,1,0:T(8,128)S(1)} %get-tuple-element.74), channel_id=1, source_target_pairs={{0,8},{8,16},{16,24},{1,9},{9,17},{17,25},{2,10},{10,18},{18,26},{... | collective-permute-start | bytes 98312 | tf_op jit(solution)/shard_map/ppermute | solution.py:17
  114.4 5.8 %collective-permute-start.7 = (f32[1,64,128]{2,1,0:T(8,128)S(1)}, f32[1,64,128]{2,1,0:T(8,128)S(1)}, u32[]{:S(2)}, u32[]{:S(2)}) collective-permute-start(f32[1,64,128]{2,1,0:T(8,128)S(1)} %get-tuple-element.75), channel_id=1, source_target_pairs={{8,0},{16,8},{24,16},{9,1},{17,9},{25,17},{10,2},{18,10},{26,18},{... | collective-permute-start | bytes 98312 | tf_op jit(solution)/shard_map/ppermute | solution.py:19
  116.0 8.6 %copy-start.28 = (f32[1,64,128]{2,1,0:T(8,128)}, f32[1,64,128]{2,1,0:T(8,128)S(1)}, u32[]{:S(2)}) copy-start(f32[1,64,128]{2,1,0:T(8,128)S(1)} %collective-permute-done.6) | copy-start | bytes 98308
  120.2 4.4 %copy-start.30 = (f32[1,64,128]{2,1,0:T(8,128)}, f32[1,64,128]{2,1,0:T(8,128)S(1)}, u32[]{:S(2)}) copy-start(f32[1,64,128]{2,1,0:T(8,128)S(1)} %collective-permute-done.7) | copy-start | bytes 98308
  120.3 2.6 collective-permute-start.8
  121.6 3.1 collective-permute-start.9
  132.0 11.6 %collective-permute-start.11 = (f32[34,66,1]{1,2,0:T(1,128)}, f32[34,66,1]{1,2,0:T(1,128)}, u32[]{:S(2)}, u32[]{:S(2)}) collective-permute-start(f32[34,66,1]{1,2,0:T(1,128)} %copy.22), channel_id=1, source_target_pairs={{1,0},{2,1},{3,2},{5,4},{6,5},{7,6},{9,8},{10,9},{11,10},{13,12},{... | collective-permute-start | bytes 26936 | tf_op jit(solution)/shard_map/ppermute | solution.py:19
  133.3 8.0 %collective-permute-start.10 = (f32[34,66,1]{1,2,0:T(1,128)}, f32[34,66,1]{1,2,0:T(1,128)}, u32[]{:S(2)}, u32[]{:S(2)}) collective-permute-start(f32[34,66,1]{1,2,0:T(1,128)} %copy.20), channel_id=1, source_target_pairs={{0,1},{1,2},{2,3},{4,5},{5,6},{6,7},{8,9},{9,10},{10,11},{12,13},{... | collective-permute-start | bytes 26936 | tf_op jit(solution)/shard_map/ppermute | solution.py:17
  146.0 4.2 %copy-start.22 = (f32[32,64,128]{2,1,0:T(8,128)S(1)}, f32[32,64,128]{2,1,0:T(8,128)}, u32[]{:S(2)}) copy-start(f32[32,64,128]{2,1,0:T(8,128)} %get-tuple-element.30) | copy-start | bytes 3145732
  146.0 4.2 %copy-start.29 = (f32[1,64,128]{2,1,0:T(8,128)S(1)}, f32[1,64,128]{2,1,0:T(8,128)}, u32[]{:S(2)}) copy-start(f32[1,64,128]{2,1,0:T(8,128)} %copy-done.28) | copy-start | bytes 98308
  146.0 4.2 %copy-start.31 = (f32[1,64,128]{2,1,0:T(8,128)S(1)}, f32[1,64,128]{2,1,0:T(8,128)}, u32[]{:S(2)}) copy-start(f32[1,64,128]{2,1,0:T(8,128)} %copy-done.30) | copy-start | bytes 98308
  150.2 9.8 %copy-start.17 = (f32[32,64,128]{2,1,0:T(8,128)S(1)}, f32[32,64,128]{2,1,0:T(8,128)}, u32[]{:S(2)}) copy-start(f32[32,64,128]{2,1,0:T(8,128)} %get-tuple-element.27) | copy-start | bytes 3145732
  160.0 9.5 %copy-start.10 = (f32[32,64,128]{2,1,0:T(8,128)}, f32[32,64,128]{2,1,0:T(8,128)S(1)}, u32[]{:S(2)}) copy-start(f32[32,64,128]{2,1,0:T(8,128)S(1)} %get-tuple-element.25) | copy-start | bytes 3145732
  160.1 8.7 %copy-start.6 = (f32[32,64,128]{2,1,0:T(8,128)}, f32[32,64,128]{2,1,0:T(8,128)S(1)}, u32[]{:S(2)}) copy-start(f32[32,64,128]{2,1,0:T(8,128)S(1)} %div.32) | copy-start | bytes 3145732
  160.2 4.4 %collective-permute-start.12 = (f32[1,64,128]{2,1,0:T(8,128)S(1)}, f32[1,64,128]{2,1,0:T(8,128)S(1)}, u32[]{:S(2)}, u32[]{:S(2)}) collective-permute-start(f32[1,64,128]{2,1,0:T(8,128)S(1)} %get-tuple-element.72), channel_id=1, source_target_pairs={{0,8},{8,16},{16,24},{1,9},{9,17},{17,25},{2,10},{10,18},{18,26},{... | collective-permute-start | bytes 98312 | tf_op jit(solution)/shard_map/ppermute | solution.py:17
  163.0 5.8 %collective-permute-start.13 = (f32[1,64,128]{2,1,0:T(8,128)S(1)}, f32[1,64,128]{2,1,0:T(8,128)S(1)}, u32[]{:S(2)}, u32[]{:S(2)}) collective-permute-start(f32[1,64,128]{2,1,0:T(8,128)S(1)} %get-tuple-element.73), channel_id=1, source_target_pairs={{8,0},{16,8},{24,16},{9,1},{17,9},{25,17},{10,2},{18,10},{26,18},{... | collective-permute-start | bytes 98312 | tf_op jit(solution)/shard_map/ppermute | solution.py:19
  164.6 4.9 %copy-start.24 = (f32[1,64,128]{2,1,0:T(8,128)}, f32[1,64,128]{2,1,0:T(8,128)S(1)}, u32[]{:S(2)}) copy-start(f32[1,64,128]{2,1,0:T(8,128)S(1)} %collective-permute-done.12) | copy-start | bytes 98308
  169.4 45.5 %collective-permute-start.14 = (f32[34,1,128]{2,1,0:T(1,128)}, f32[34,1,128]{2,1,0:T(1,128)}, u32[]{:S(2)}, u32[]{:S(2)}) collective-permute-start(f32[34,1,128]{2,1,0:T(1,128)} %get-tuple-element.64), channel_id=1, source_target_pairs={{0,4},{1,5},{2,6},{3,7},{8,12},{9,13},{10,14},{11,15},{16,20},{17,... | collective-permute-start | bytes 52232 | tf_op jit(solution)/shard_map/ppermute | solution.py:17
  171.3 43.6 %collective-permute-start.15 = (f32[34,1,128]{2,1,0:T(1,128)}, f32[34,1,128]{2,1,0:T(1,128)}, u32[]{:S(2)}, u32[]{:S(2)}) collective-permute-start(f32[34,1,128]{2,1,0:T(1,128)} %get-tuple-element.65), channel_id=1, source_target_pairs={{4,0},{5,1},{6,2},{7,3},{12,8},{13,9},{14,10},{15,11},{20,16},{21,... | collective-permute-start | bytes 52232 | tf_op jit(solution)/shard_map/ppermute | solution.py:19
  222.9 12.0 %collective-permute-start.17 = (f32[34,66,1]{1,2,0:T(1,128)}, f32[34,66,1]{1,2,0:T(1,128)}, u32[]{:S(2)}, u32[]{:S(2)}) collective-permute-start(f32[34,66,1]{1,2,0:T(1,128)} %copy.26), channel_id=1, source_target_pairs={{1,0},{2,1},{3,2},{5,4},{6,5},{7,6},{9,8},{10,9},{11,10},{13,12},{... | collective-permute-start | bytes 26936 | tf_op jit(solution)/shard_map/ppermute | solution.py:19
  224.1 8.4 %collective-permute-start.16 = (f32[34,66,1]{1,2,0:T(1,128)}, f32[34,66,1]{1,2,0:T(1,128)}, u32[]{:S(2)}, u32[]{:S(2)}) collective-permute-start(f32[34,66,1]{1,2,0:T(1,128)} %copy.24), channel_id=1, source_target_pairs={{0,1},{1,2},{2,3},{4,5},{5,6},{6,7},{8,9},{9,10},{10,11},{12,13},{... | collective-permute-start | bytes 26936 | tf_op jit(solution)/shard_map/ppermute | solution.py:17
  237.2 4.1 %copy-start.4 = (f32[34,66,130]{2,1,0:T(8,128)S(1)}, f32[34,66,130]{2,1,0:T(8,128)}, u32[]{:S(2)}) copy-start(f32[34,66,130]{2,1,0:T(8,128)} %get-tuple-element.36) | copy-start | bytes 3500644
  237.2 4.2 %copy-start.7 = (f32[32,64,128]{2,1,0:T(8,128)S(1)}, f32[32,64,128]{2,1,0:T(8,128)}, u32[]{:S(2)}) copy-start(f32[32,64,128]{2,1,0:T(8,128)} %copy-done.6) | copy-start | bytes 3145732
  237.2 4.5 %copy-start.11 = (f32[32,64,128]{2,1,0:T(8,128)S(1)}, f32[32,64,128]{2,1,0:T(8,128)}, u32[]{:S(2)}) copy-start(f32[32,64,128]{2,1,0:T(8,128)} %copy-done.10) | copy-start | bytes 3145732
  237.2 4.8 %copy-start.18 = (f32[32,64,128]{2,1,0:T(8,128)S(1)}, f32[32,64,128]{2,1,0:T(8,128)}, u32[]{:S(2)}) copy-start(f32[32,64,128]{2,1,0:T(8,128)} %get-tuple-element.27) | copy-start | bytes 3145732
  237.2 4.8 %copy-start.25 = (f32[1,64,128]{2,1,0:T(8,128)S(1)}, f32[1,64,128]{2,1,0:T(8,128)}, u32[]{:S(2)}) copy-start(f32[1,64,128]{2,1,0:T(8,128)} %copy-done.24) | copy-start | bytes 98308
  237.2 4.8 %copy-start.27 = (f32[1,64,128]{2,1,0:T(8,128)S(1)}, f32[1,64,128]{2,1,0:T(8,128)}, u32[]{:S(2)}) copy-start(f32[1,64,128]{2,1,0:T(8,128)} %copy-done.26) | copy-start | bytes 98308
  242.0 16.2 %copy-start.23 = (f32[32,64,128]{2,1,0:T(8,128)S(1)}, f32[32,64,128]{2,1,0:T(8,128)}, u32[]{:S(2)}) copy-start(f32[32,64,128]{2,1,0:T(8,128)} %param.5) | copy-start | bytes 3145732
  251.5 8.0 %copy-start.14 = (f32[32,64,128]{2,1,0:T(8,128)}, f32[32,64,128]{2,1,0:T(8,128)S(1)}, u32[]{:S(2)}) copy-start(f32[32,64,128]{2,1,0:T(8,128)S(1)} %get-tuple-element.23) | copy-start | bytes 3145732
  251.5 8.0 %copy-start.19 = (f32[32,64,128]{2,1,0:T(8,128)}, f32[32,64,128]{2,1,0:T(8,128)S(1)}, u32[]{:S(2)}) copy-start(f32[32,64,128]{2,1,0:T(8,128)S(1)} %get-tuple-element.24) | copy-start | bytes 3145732
  252.2 52.9 %collective-permute-start.18 = (f32[1,64,128]{2,1,0:T(8,128)}, f32[1,64,128]{2,1,0:T(8,128)}, u32[]{:S(2)}, u32[]{:S(2)}) collective-permute-start(f32[1,64,128]{2,1,0:T(8,128)} %get-tuple-element.70), channel_id=1, source_target_pairs={{0,8},{8,16},{16,24},{1,9},{9,17},{17,25},{2,10},{10,18},{18,26},{... | collective-permute-start | bytes 98312 | tf_op jit(solution)/shard_map/ppermute | solution.py:17
  257.0 48.2 %collective-permute-start.19 = (f32[1,64,128]{2,1,0:T(8,128)}, f32[1,64,128]{2,1,0:T(8,128)}, u32[]{:S(2)}, u32[]{:S(2)}) collective-permute-start(f32[1,64,128]{2,1,0:T(8,128)} %get-tuple-element.71), channel_id=1, source_target_pairs={{8,0},{16,8},{24,16},{9,1},{17,9},{25,17},{10,2},{18,10},{26,18},{... | collective-permute-start | bytes 98312 | tf_op jit(solution)/shard_map/ppermute | solution.py:19
  306.1 6.8 %collective-permute-start.20 = (f32[34,1,128]{2,1,0:T(1,128)S(1)}, f32[34,1,128]{2,1,0:T(1,128)S(1)}, u32[]{:S(2)}, u32[]{:S(2)}) collective-permute-start(f32[34,1,128]{2,1,0:T(1,128)S(1)} %get-tuple-element.60), channel_id=1, source_target_pairs={{0,4},{1,5},{2,6},{3,7},{8,12},{9,13},{10,14},{11,15},{16,20},{17,... | collective-permute-start | bytes 52232 | tf_op jit(solution)/shard_map/ppermute | solution.py:17
  307.4 5.5 %copy-start.15 = (f32[32,64,128]{2,1,0:T(8,128)S(1)}, f32[32,64,128]{2,1,0:T(8,128)}, u32[]{:S(2)}) copy-start(f32[32,64,128]{2,1,0:T(8,128)} %copy-done.14) | copy-start | bytes 3145732
  307.4 5.5 %collective-permute-start.21 = (f32[34,1,128]{2,1,0:T(1,128)S(1)}, f32[34,1,128]{2,1,0:T(1,128)S(1)}, u32[]{:S(2)}, u32[]{:S(2)}) collective-permute-start(f32[34,1,128]{2,1,0:T(1,128)S(1)} %get-tuple-element.61), channel_id=1, source_target_pairs={{4,0},{5,1},{6,2},{7,3},{12,8},{13,9},{14,10},{15,11},{20,16},{21,... | collective-permute-start | bytes 52232 | tf_op jit(solution)/shard_map/ppermute | solution.py:19
  320.4 12.0 %collective-permute-start.23 = (f32[34,66,1]{1,2,0:T(1,128)}, f32[34,66,1]{1,2,0:T(1,128)}, u32[]{:S(2)}, u32[]{:S(2)}) collective-permute-start(f32[34,66,1]{1,2,0:T(1,128)} %copy.30), channel_id=1, source_target_pairs={{1,0},{2,1},{3,2},{5,4},{6,5},{7,6},{9,8},{10,9},{11,10},{13,12},{... | collective-permute-start | bytes 26936 | tf_op jit(solution)/shard_map/ppermute | solution.py:19
  321.7 8.4 %collective-permute-start.22 = (f32[34,66,1]{1,2,0:T(1,128)}, f32[34,66,1]{1,2,0:T(1,128)}, u32[]{:S(2)}, u32[]{:S(2)}) collective-permute-start(f32[34,66,1]{1,2,0:T(1,128)} %copy.28), channel_id=1, source_target_pairs={{0,1},{1,2},{2,3},{4,5},{5,6},{6,7},{8,9},{9,10},{10,11},{12,13},{... | collective-permute-start | bytes 26936 | tf_op jit(solution)/shard_map/ppermute | solution.py:17
  334.7 4.2 %copy-start.8 = (f32[32,64,128]{2,1,0:T(8,128)S(1)}, f32[32,64,128]{2,1,0:T(8,128)}, u32[]{:S(2)}) copy-start(f32[32,64,128]{2,1,0:T(8,128)} %copy-done.6) | copy-start | bytes 3145732
  334.7 4.5 %copy-start.12 = (f32[32,64,128]{2,1,0:T(8,128)S(1)}, f32[32,64,128]{2,1,0:T(8,128)}, u32[]{:S(2)}) copy-start(f32[32,64,128]{2,1,0:T(8,128)} %copy-done.10) | copy-start | bytes 3145732
  334.8 4.8 %copy-start.16 = (f32[32,64,128]{2,1,0:T(8,128)S(1)}, f32[32,64,128]{2,1,0:T(8,128)}, u32[]{:S(2)}) copy-start(f32[32,64,128]{2,1,0:T(8,128)} %copy-done.14) | copy-start | bytes 3145732
  (12 other events, 38.1 us)
where the time goes:
time: 400 us; the launch traced here: 398 us
  blocking collectives  123 us (31%)
  other arithmetic  106 us (26%)
  local copies, waits for them, and re-layouts  81.7 us (20%)
  starting transfers between devices  57 us (14%)
  waiting for transfers between devices  20.8 us (5%)
  between operations  10.1 us (3%)
    psum x3, blocking collectives, local(): lax.psum((jnp.sum(residual * precond), jnp.sum(applied * precond)), ('gx'...  123 us
    concatenate x11, other arithmetic, with_halo(): jnp.concatenate([lax.ppermute(tail, axis, [(i, (i + 1) % count) for i in...  45.8 us
    ppermute x12, starting transfers between devices, with_halo(): lax.ppermute(tail, axis, [(i, (i + 1) % count) for i in range(ends)])  41 us
    slice x12, local copies, waits for them, and re-layouts, with_halo(): lax.slice_in_dim(cells, cells.shape[dim] - width, cells.shape[dim], axis=...  31 us
    reduce_sum x3, other arithmetic, local(): jnp.sum(applied * precond)  21.8 us
    ppermute x12, waiting for transfers between devices, with_halo(): lax.ppermute(head, axis, [((i + 1) % count, i) for i in range(ends)])  18.5 us
    ppermute x12, starting transfers between devices, with_halo(): lax.ppermute(head, axis, [((i + 1) % count, i) for i in range(ends)])  16 us
    div x1, other arithmetic, local(): precond = residual / diag  13.2 us
  transfers between devices with their start and end apart: 24, of which 9 were waited for; matrix products, arithmetic and copies ran while one was open for 8% of the time, Pallas kernels for 0%

commit v1 on v0

--- a/solution.py
+++ b/solution.py
@@ -132,7 +132,7 @@
     direction = precond
     for step in range(ITERS):
         gamma, delta = lax.psum(
-            (jnp.sum(residual * precond), jnp.sum(applied * precond)), ("gx", "gy", "gz")
+            lax.psum((jnp.sum(residual * precond), jnp.sum(applied * precond)), ("gy", "gz")), "gx"
         )
         if step + 1 < ITERS:
             scaled = applied / diag

time: 400 us -> 356 us (0.89)
  blocking collectives: 123 us -> 80.3 us
    psum x3 -> x6, blocking collectives: 123 us -> 80.3 us  [the longest x3 50.3 us: local(): lax.psum((jnp.sum(residual * precond), jnp.sum(applied * precond)), ('gy'...]
  transfers between devices with their start and end apart: 24 -> 24, of which waited for: 9 -> 9; matrix products, arithmetic and copies ran while one was open for 8% -> 9% of each run, Pallas kernels for 0% -> 0%
where the time goes in v1:
time: 356 us; the launch traced here: 354 us
  other arithmetic  106 us (30%)
  local copies, waits for them, and re-layouts  81.5 us (23%)
  blocking collectives  80.3 us (23%)
  starting transfers between devices  55.5 us (16%)
  waiting for transfers between devices  20.8 us (6%)
  between operations  9.92 us (3%)
    psum x3, blocking collectives, local(): lax.psum((jnp.sum(residual * precond), jnp.sum(applied * precond)), ('gy'...  50.3 us
    concatenate x11, other arithmetic, with_halo(): jnp.concatenate([lax.ppermute(tail, axis, [(i, (i + 1) % count) for i in...  46 us
    ppermute x12, starting transfers between devices, with_halo(): lax.ppermute(tail, axis, [(i, (i + 1) % count) for i in range(ends)])  39.7 us
    slice x12, local copies, waits for them, and re-layouts, with_halo(): lax.slice_in_dim(cells, cells.shape[dim] - width, cells.shape[dim], axis=...  31 us
    psum x3, blocking collectives, local(): lax.psum(lax.psum((jnp.sum(residual * precond), jnp.sum(applied * precond...  30 us
    reduce_sum x3, other arithmetic, local(): jnp.sum(applied * precond)  21.8 us
    ppermute x12, waiting for transfers between devices, with_halo(): lax.ppermute(head, axis, [((i + 1) % count, i) for i in range(ends)])  18.5 us
    ppermute x12, starting transfers between devices, with_halo(): lax.ppermute(head, axis, [((i + 1) % count, i) for i in range(ends)])  15.8 us
  transfers between devices with their start and end apart: 24, of which 9 were waited for; matrix products, arithmetic and copies ran while one was open for 9% of the time, Pallas kernels for 0%

profile of v1, /device:TPU:0, one launch (start us, length us, event | category | flops | bytes accessed | tf_op | source)
XLA Modules:
  0.0 354.1 jit_solution(11190124885855075967)
XLA Ops:
  3.3 4.1 %multiply_add_fusion = f32[7,32,64,128]{3,2,1,0:T(8,128)S(1)} fusion(f32[7]{0:T(128)S(1)} %get-tuple-element.15, f32[32,64,128]{2,1,0:T(8,128)S(1)} %get-tuple-element.89, f32[7]{0:T(128)S(1)} %get-tuple-element.16, f32[32,64,128]{2,1,0:T(8,128)S(1)} %get-tuple-element.88, f32[7]{0:T(128)S(1)} %get-tuple-element.10, f32[32,64,128]{2,1,0:T(8,128)S(1)} %get-tuple-element.87, ...), kind=kLoop, calls=%fused_computation.2 | loop fusion | flops 27525120 | bytes 15728864 | tf_op jit(solution)/shard_map/add | solution.py:111
  7.5 4.9 %collective-permute-start = (f32[6,1,64,128]{3,2,1,0:T(8,128)S(1)}, f32[6,1,64,128]{3,2,1,0:T(8,128)S(1)}, u32[]{:S(2)}, u32[]{:S(2)}) collective-permute-start(f32[6,1,64,128]{3,2,1,0:T(8,128)S(1)} %get-tuple-element.48), channel_id=1, source_target_pairs={{0,8},{8,16},{16,24},{1,9},{9,17},{17,25},{2,10},{10,18},{18,26},{... | collective-permute-start | bytes 589832 | tf_op jit(solution)/shard_map/ppermute | solution.py:17
  16.5 6.2 %collective-permute-done.1 = f32[6,1,64,128]{3,2,1,0:T(8,128)S(1)} collective-permute-done((f32[6,1,64,128]{3,2,1,0:T(8,128)S(1)}, f32[6,1,64,128]{3,2,1,0:T(8,128)S(1)}, u32[]{:S(2)}, u32[]{:S(2)}) %collective-permute-start.1) | collective-permute-done | bytes 196640 | tf_op jit(solution)/shard_map/ppermute | solution.py:19
  27.3 3.6 %pad_maximum_fusion.1 = f32[6,34,66,128]{3,2,1,0:T(8,128)} fusion(f32[6,34,1,128]{3,2,1,0:T(1,128)S(1)} %collective-permute-done.3, f32[6,1,64,128]{3,2,1,0:T(8,128)S(1)} %collective-permute-done.1, f32[6,32,64,128]{3,2,1,0:T(8,128)S(1)} %slice.740, f32[6,1,64,128]{3,2,1,0:T(8,128)S(1)} %collective-permute-done, f32[6,34,1,128]{3,2,1,0:T(1,128)S(1)} %collective-permute-done.2), kind=kLoop, calls=%fused_computation.1 | loop fusion | flops 6893568 | bytes 13787136 | tf_op jit(solution)/shard_map/concatenate | solution.py:15
  30.9 12.6 %fusion.111 = (f32[6,34,66,1]{3,2,1,0:T(8,128)}, f32[6,34,66,1]{3,2,1,0:T(8,128)}) fusion(f32[6,34,66,128]{3,2,1,0:T(8,128)} %pad_maximum_fusion.1), kind=kLoop, calls=%fused_computation.239 | loop fusion | bytes 215424 | tf_op jit(solution)/shard_map/slice | solution.py:14
  43.4 5.1 %copy.16 = f32[6,34,66,1]{2,3,1,0:T(1,128)S(1)} copy(f32[6,34,66,1]{3,2,1,0:T(8,128)} %get-tuple-element.46) | data formatting | bytes 107712 | tf_op jit(solution)/shard_map/slice | solution.py:14
  48.6 3.5 collective-permute-start.4
  52.1 5.1 %copy.17 = f32[6,34,66,1]{2,3,1,0:T(1,128)S(1)} copy(f32[6,34,66,1]{3,2,1,0:T(8,128)} %get-tuple-element.47) | data formatting | bytes 107712 | tf_op jit(solution)/shard_map/slice | solution.py:13
  58.7 4.9 %copy.18 = f32[6,34,66,1]{3,2,1,0:T(8,128)} copy(f32[6,34,66,1]{2,3,1,0:T(1,128)S(1)} %collective-permute-done.4) | data formatting | bytes 107712 | tf_op jit(solution)/shard_map/ppermute | solution.py:17
  63.8 4.6 %copy.19 = f32[6,34,66,1]{3,2,1,0:T(8,128)} copy(f32[6,34,66,1]{2,3,1,0:T(1,128)S(1)} %collective-permute-done.5) | data formatting | bytes 107712 | tf_op jit(solution)/shard_map/ppermute | solution.py:19
  68.4 19.0 %pad_maximum_fusion = f32[6,34,66,130]{3,2,1,0:T(8,128)} fusion(f32[6,34,66,1]{3,2,1,0:T(8,128)} %copy.19, f32[6,34,1,128]{3,2,1,0:T(1,128)S(1)} %collective-permute-done.3, f32[6,1,64,128]{3,2,1,0:T(8,128)S(1)} %collective-permute-done.1, f32[6,32,64,128]{3,2,1,0:T(8,128)} %copy-done.9, f32[6,1,64,128]{3,2,1,0:T(8,128)S(1)} %collective-permute-done, ...), kind=kLoop, calls=%fused_computation | loop fusion | flops 10501920 | bytes 14002560 | tf_op jit(solution)/shard_map/concatenate | solution.py:15
  87.4 10.2 %slice_bitcast_fusion.2 = (f32[34,66,130]{2,1,0:T(8,128)S(1)}, f32[34,66,130]{2,1,0:T(8,128)}, f32[34,66,130]{2,1,0:T(8,128)}, f32[34,66,130]{2,1,0:T(8,128)}, f...) fusion(f32[6,34,66,130]{3,2,1,0:T(8,128)} %pad_maximum_fusion), kind=kLoop, calls=%fused_computation.5 | loop fusion | bytes 14002560 | tf_op jit(solution)/shard_map/squeeze | solution.py:71
  97.5 13.1 %fusion.104 = (f32[32,64,128]{2,1,0:T(8,128)S(1)}, f32[32,64,128]{2,1,0:T(8,128)}, f32[32,64,128]{2,1,0:T(8,128)}, f32[32,64,128]{2,1,0:T(8,128)}, f32[32,64,128...) fusion(f32[32,64,128]{2,1,0:T(8,128)} %param.5, ...), kind=kLoop, calls=%fused_computation.238 | loop fusion | flops 4980736 | bytes 19922944 | tf_op jit(solution)/shard_map/div | solution.py:128
  110.7 3.4 collective-permute-start.6
  115.7 4.2 %collective-permute-done.7 = f32[1,64,128]{2,1,0:T(8,128)S(1)} collective-permute-done((f32[1,64,128]{2,1,0:T(8,128)S(1)}, f32[1,64,128]{2,1,0:T(8,128)S(1)}, u32[]{:S(2)}, u32[]{:S(2)}) %collective-permute-start.7) | collective-permute-done | bytes 32800 | tf_op jit(solution)/shard_map/ppermute | solution.py:19
  126.9 2.4 copy.20
  129.3 2.4 copy.22
  132.9 5.5 %collective-permute-start.10 = (f32[34,66,1]{1,2,0:T(1,128)}, f32[34,66,1]{1,2,0:T(1,128)}, u32[]{:S(2)}, u32[]{:S(2)}) collective-permute-start(f32[34,66,1]{1,2,0:T(1,128)} %copy.20), channel_id=1, source_target_pairs={{0,1},{1,2},{2,3},{4,5},{5,6},{6,7},{8,9},{9,10},{10,11},{12,13},{... | collective-permute-start | bytes 26936 | tf_op jit(solution)/shard_map/ppermute | solution.py:17
  138.5 2.5 maximum_maximum_fusion.3
  141.0 2.3 copy.21
  143.3 2.4 copy.23
  145.7 3.8 %maximum_maximum_fusion = (f32[34,66,129]{2,1,0:T(8,128)S(1)}, f32[34,66,129]{2,1,0:T(8,128)S(1)}) fusion(f32[34,1,128]{2,1,0:T(1,128)} %copy-done.35, f32[1,64,128]{2,1,0:T(8,128)} %copy-done.30, f32[32,64,128]{2,1,0:T(8,128)S(1)} %get-tuple-element.32, f32[1,64,128]{2,1,0:T(8,128)} %copy-done.28, f32[34,1,128]{2,1,0:T(1,128)} %copy-done.33, ...), kind=kLoop, calls=%fused_computation.9 | loop fusion | flops 2894760 | bytes 3482688 | tf_op jit(solution)/shard_map/concatenate | solution.py:15
  149.8 9.8 %multiply_reduce_fusion.3 = (f32[]{:T(128)}, f32[]{:T(128)}, f32[32,64,128]{2,1,0:T(8,128)S(1)}) fusion(f32[32,64,128]{2,1,0:T(8,128)S(1)} %get-tuple-element.32, f32[32,64,128]{2,1,0:T(8,128)} %param.5, f32[34,66,129]{2,1,0:T(8,128)S(1)} %get-tuple-element.63, f32[34,66,130]{2,1,0:T(8,128)S(1)} %copy-done, f32[34,66,129]{2,1,0:T(8,128)S(1)} %get-tuple-element.62, ...), kind=kLoop, calls=%fused_computation.206 | loop fusion | flops 19136512 | bytes 43057160 | tf_op jit(solution)/shard_map/reduce_sum | solution.py:135
  159.9 2.8 collective-permute-start.12
  164.3 4.2 %collective-permute-done.13 = f32[1,64,128]{2,1,0:T(8,128)S(1)} collective-permute-done((f32[1,64,128]{2,1,0:T(8,128)S(1)}, f32[1,64,128]{2,1,0:T(8,128)S(1)}, u32[]{:S(2)}, u32[]{:S(2)}) %collective-permute-start.13) | collective-permute-done | bytes 32800 | tf_op jit(solution)/shard_map/ppermute | solution.py:19
  172.3 19.6 %all-reduce.2 = (f32[]{:T(128)}, f32[]{:T(128)}) all-reduce(f32[]{:T(128)} %get-tuple-element.8, f32[]{:T(128)} %get-tuple-element.7), channel_id=1, replica_groups=mesh['gx'=4,'gy'=2,'gz'=4] {'gy','gz'}, use_global_device_ids=true, to_apply=%region_1.0 | all-reduce | flops 2 | bytes 16 | tf_op jit(solution)/shard_map/psum | solution.py:135
  191.9 9.1 %all-reduce.5 = (f32[]{:T(128)}, f32[]{:T(128)}) all-reduce(f32[]{:T(128)} %get-tuple-element.21, f32[]{:T(128)} %get-tuple-element.22), channel_id=1, replica_groups=mesh['gx'=4,'gy'=2,'gz'=4] {'gx'}, use_global_device_ids=true, to_apply=%region_2.0 | all-reduce | flops 2 | bytes 16 | tf_op jit(solution)/shard_map/psum | solution.py:134
  205.5 2.4 copy.24
  207.9 2.4 copy.26
  211.5 5.1 %collective-permute-start.16 = (f32[34,66,1]{1,2,0:T(1,128)}, f32[34,66,1]{1,2,0:T(1,128)}, u32[]{:S(2)}, u32[]{:S(2)}) collective-permute-start(f32[34,66,1]{1,2,0:T(1,128)} %copy.24), channel_id=1, source_target_pairs={{0,1},{1,2},{2,3},{4,5},{5,6},{6,7},{8,9},{9,10},{10,11},{12,13},{... | collective-permute-start | bytes 26936 | tf_op jit(solution)/shard_map/ppermute | solution.py:17
  216.6 3.3 maximum_maximum_fusion.4
  222.2 2.4 copy.27
  224.6 4.2 %maximum_maximum_fusion.1 = (f32[34,66,129]{2,1,0:T(8,128)S(1)}, f32[34,66,129]{2,1,0:T(8,128)S(1)}) fusion(f32[34,1,128]{2,1,0:T(1,128)} %collective-permute-done.15, f32[1,64,128]{2,1,0:T(8,128)} %copy-done.26, f32[32,64,128]{2,1,0:T(8,128)} %copy-done.6, f32[1,64,128]{2,1,0:T(8,128)} %copy-done.24, f32[34,1,128]{2,1,0:T(1,128)} %collective-permute-done.14, ...), kind=kLoop, calls=%fused_computation.11 | loop fusion | flops 2894760 | bytes 3482688 | tf_op jit(solution)/shard_map/concatenate | solution.py:15
  229.4 9.6 %fusion.101 = (f32[32,64,128]{2,1,0:T(8,128)S(1)}, f32[32,64,128]{2,1,0:T(8,128)S(1)}) fusion(f32[32,64,128]{2,1,0:T(8,128)S(1)} %copy-done.18, f32[32,64,128]{2,1,0:T(8,128)S(1)} %copy-done.11, f32[]{:T(128)S(6)} %div.31, f32[34,66,129]{2,1,0:T(8,128)S(1)} %get-tuple-element.61, f32[34,66,130]{2,1,0:T(8,128)S(1)} %copy-done.1, ...), kind=kLoop, calls=%fused_computation.217 | loop fusion | flops 18874368 | bytes 45154308 | tf_op jit(solution)/shard_map/div | solution.py:138
  239.7 3.6 %collective-permute-start.18 = (f32[1,64,128]{2,1,0:T(8,128)}, f32[1,64,128]{2,1,0:T(8,128)}, u32[]{:S(2)}, u32[]{:S(2)}) collective-permute-start(f32[1,64,128]{2,1,0:T(8,128)} %get-tuple-element.76), channel_id=1, source_target_pairs={{0,8},{8,16},{16,24},{1,9},{9,17},{17,25},{2,10},{10,18},{18,26},{... | collective-permute-start | bytes 98312 | tf_op jit(solution)/shard_map/ppermute | solution.py:17
  245.8 14.7 %all-reduce.1 = (f32[]{:T(128)}, f32[]{:T(128)}) all-reduce(f32[]{:T(128)} %get-tuple-element.6, f32[]{:T(128)} %get-tuple-element.5), channel_id=1, replica_groups=mesh['gx'=4,'gy'=2,'gz'=4] {'gy','gz'}, use_global_device_ids=true, to_apply=%region_7.0 | all-reduce | flops 2 | bytes 16 | tf_op jit(solution)/shard_map/psum | solution.py:135
  260.5 10.8 %all-reduce.4 = (f32[]{:T(128)}, f32[]{:T(128)}) all-reduce(f32[]{:T(128)} %get-tuple-element.19, f32[]{:T(128)} %get-tuple-element.20), channel_id=1, replica_groups=mesh['gx'=4,'gy'=2,'gz'=4] {'gx'}, use_global_device_ids=true, to_apply=%region_8.0 | all-reduce | flops 2 | bytes 16 | tf_op jit(solution)/shard_map/psum | solution.py:134
  279.5 3.7 %multiply_reduce_fusion = f32[]{:T(128)} fusion(f32[32,64,128]{2,1,0:T(8,128)} %copy-done.10, f32[32,64,128]{2,1,0:T(8,128)} %param.5, f32[]{:T(128)S(6)} %div.33, f32[]{:T(128)S(6)} %div.35, f32[]{:T(128)S(6)} %div.31, f32[32,64,128]{2,1,0:T(8,128)} %copy-done.19, f32[32,64,128]{2,1,0:T(8,128)} %copy-done.6, f32[32,64,128]{2,1,0:T(8,128)} %get-tuple-element.33, ...), kind=kLoop, calls=%fused_computation.199 | loop fusion | flops 4456447 | bytes 6291472 | tf_op jit(solution)/shard_map/reduce_sum | solution.py:135
  286.0 2.4 copy.28
  288.3 2.4 copy.30
  292.0 5.1 %collective-permute-start.22 = (f32[34,66,1]{1,2,0:T(1,128)}, f32[34,66,1]{1,2,0:T(1,128)}, u32[]{:S(2)}, u32[]{:S(2)}) collective-permute-start(f32[34,66,1]{1,2,0:T(1,128)} %copy.28), channel_id=1, source_target_pairs={{0,1},{1,2},{2,3},{4,5},{5,6},{6,7},{8,9},{9,10},{10,11},{12,13},{... | collective-permute-start | bytes 26936 | tf_op jit(solution)/shard_map/ppermute | solution.py:17
  297.1 3.2 maximum_maximum_fusion.5
  302.6 2.4 copy.31
  305.0 4.1 %maximum_maximum_fusion.2 = (f32[34,66,129]{2,1,0:T(8,128)S(1)}, f32[34,66,129]{2,1,0:T(8,128)S(1)}) fusion(f32[34,1,128]{2,1,0:T(1,128)} %copy-done.34, f32[1,64,128]{2,1,0:T(8,128)} %collective-permute-done.19, f32[32,64,128]{2,1,0:T(8,128)} %copy-done.14, f32[1,64,128]{2,1,0:T(8,128)} %collective-permute-done.18, f32[34,1,128]{2,1,0:T(1,128)} %copy-done.32, ...), kind=kLoop, calls=%fused_computation.13 | loop fusion | flops 2894760 | bytes 3482688 | tf_op jit(solution)/shard_map/concatenate | solution.py:15
  309.8 10.8 %fusion.5 = f32[]{:T(128)} fusion(f32[34,66,129]{2,1,0:T(8,128)S(1)} %get-tuple-element.59, f32[34,66,129]{2,1,0:T(8,128)S(1)} %get-tuple-element.58, f32[34,65,128]{2,1,0:T(8,128)} %get-tuple-element.65, f32[34,65,128]{2,1,0:T(8,128)} %get-tuple-element.64, f32[32,64,128]{2,1,0:T(8,128)} %get-tuple-element.39, f32[32,64,128]{2,1,0:T(8,128)S(1)} %copy-done.16, ...), kind=kLoop, calls=%fused_computation.30 | loop fusion | flops 22020096 | bytes 46202896 | tf_op jit(solution)/shard_map/reduce_sum | solution.py:135
  320.6 15.9 %all-reduce = (f32[]{:T(128)}, f32[]{:T(128)}) all-reduce(f32[]{:T(128)} %multiply_reduce_fusion, f32[]{:T(128)} %fusion.5), channel_id=1, replica_groups=mesh['gx'=4,'gy'=2,'gz'=4] {'gy','gz'}, use_global_device_ids=true, to_apply=%region_13.0 | all-reduce | flops 2 | bytes 16 | tf_op jit(solution)/shard_map/psum | solution.py:135
  336.5 10.2 %all-reduce.3 = (f32[]{:T(128)}, f32[]{:T(128)}) all-reduce(f32[]{:T(128)} %get-tuple-element.17, f32[]{:T(128)} %get-tuple-element.18), channel_id=1, replica_groups=mesh['gx'=4,'gy'=2,'gz'=4] {'gx'}, use_global_device_ids=true, to_apply=%region_14.0 | all-reduce | flops 2 | bytes 16 | tf_op jit(solution)/shard_map/psum | solution.py:134
  350.3 3.8 %multiply_add_fusion.1 = f32[32,64,128]{2,1,0:T(8,128)} fusion(f32[32,64,128]{2,1,0:T(8,128)S(1)} %get-tuple-element.32, f32[]{:T(128)S(6)} %div.37, f32[]{:T(128)S(6)} %div.39, f32[]{:T(128)S(6)} %div.33, f32[]{:T(128)S(6)} %div.35, f32[]{:T(128)S(6)} %div.31, f32[32,64,128]{2,1,0:T(8,128)} %copy-done.6, f32[32,64,128]{2,1,0:T(8,128)} %get-tuple-element.33, ...), kind=kLoop, calls=%fused_computation.198 | loop fusion | flops 4718592 | bytes 6291476 | tf_op jit(solution)/shard_map/add | solution.py:154
  (130 shorter events, 50.9 us)
Async XLA Ops:
  7.4 7.4 %copy-start.13 = (f32[7,32,64,128]{3,2,1,0:T(8,128)}, f32[7,32,64,128]{3,2,1,0:T(8,128)S(1)}, u32[]{:S(2)}) copy-start(f32[7,32,64,128]{3,2,1,0:T(8,128)S(1)} %multiply_add_fusion) | copy-start | bytes 22020100
  7.5 9.0 %collective-permute-start = (f32[6,1,64,128]{3,2,1,0:T(8,128)S(1)}, f32[6,1,64,128]{3,2,1,0:T(8,128)S(1)}, u32[]{:S(2)}, u32[]{:S(2)}) collective-permute-start(f32[6,1,64,128]{3,2,1,0:T(8,128)S(1)} %get-tuple-element.48), channel_id=1, source_target_pairs={{0,8},{8,16},{16,24},{1,9},{9,17},{17,25},{2,10},{10,18},{18,26},{... | collective-permute-start | bytes 589832 | tf_op jit(solution)/shard_map/ppermute | solution.py:17
  12.4 10.3 %collective-permute-start.1 = (f32[6,1,64,128]{3,2,1,0:T(8,128)S(1)}, f32[6,1,64,128]{3,2,1,0:T(8,128)S(1)}, u32[]{:S(2)}, u32[]{:S(2)}) collective-permute-start(f32[6,1,64,128]{3,2,1,0:T(8,128)S(1)} %get-tuple-element.49), channel_id=1, source_target_pairs={{8,0},{16,8},{24,16},{9,1},{17,9},{25,17},{10,2},{18,10},{26,18},{... | collective-permute-start | bytes 589832 | tf_op jit(solution)/shard_map/ppermute | solution.py:19
  14.8 12.5 %copy-start.9 = (f32[6,32,64,128]{3,2,1,0:T(8,128)}, f32[6,32,64,128]{3,2,1,0:T(8,128)S(1)}, u32[]{:S(2)}) copy-start(f32[6,32,64,128]{3,2,1,0:T(8,128)S(1)} %slice.740) | copy-start | bytes 18874372
  22.8 2.6 collective-permute-start.2
  24.1 3.2 collective-permute-start.3
  48.6 10.1 %collective-permute-start.4 = (f32[6,34,66,1]{2,3,1,0:T(1,128)S(1)}, f32[6,34,66,1]{2,3,1,0:T(1,128)S(1)}, u32[]{:S(2)}, u32[]{:S(2)}) collective-permute-start(f32[6,34,66,1]{2,3,1,0:T(1,128)S(1)} %copy.16), channel_id=1, source_target_pairs={{0,1},{1,2},{2,3},{4,5},{5,6},{6,7},{8,9},{9,10},{10,11},{12,13},{... | collective-permute-start | bytes 161576 | tf_op jit(solution)/shard_map/ppermute | solution.py:17
  57.2 6.6 %collective-permute-start.5 = (f32[6,34,66,1]{2,3,1,0:T(1,128)S(1)}, f32[6,34,66,1]{2,3,1,0:T(1,128)S(1)}, u32[]{:S(2)}, u32[]{:S(2)}) collective-permute-start(f32[6,34,66,1]{2,3,1,0:T(1,128)S(1)} %copy.17), channel_id=1, source_target_pairs={{1,0},{2,1},{3,2},{5,4},{6,5},{7,6},{9,8},{10,9},{11,10},{13,12},{... | collective-permute-start | bytes 161576 | tf_op jit(solution)/shard_map/ppermute | solution.py:19
  110.7 5.0 %collective-permute-start.6 = (f32[1,64,128]{2,1,0:T(8,128)S(1)}, f32[1,64,128]{2,1,0:T(8,128)S(1)}, u32[]{:S(2)}, u32[]{:S(2)}) collective-permute-start(f32[1,64,128]{2,1,0:T(8,128)S(1)} %get-tuple-element.80), channel_id=1, source_target_pairs={{0,8},{8,16},{16,24},{1,9},{9,17},{17,25},{2,10},{10,18},{18,26},{... | collective-permute-start | bytes 98312 | tf_op jit(solution)/shard_map/ppermute | solution.py:17
  114.1 5.8 %collective-permute-start.7 = (f32[1,64,128]{2,1,0:T(8,128)S(1)}, f32[1,64,128]{2,1,0:T(8,128)S(1)}, u32[]{:S(2)}, u32[]{:S(2)}) collective-permute-start(f32[1,64,128]{2,1,0:T(8,128)S(1)} %get-tuple-element.81), channel_id=1, source_target_pairs={{8,0},{16,8},{24,16},{9,1},{17,9},{25,17},{10,2},{18,10},{26,18},{... | collective-permute-start | bytes 98312 | tf_op jit(solution)/shard_map/ppermute | solution.py:19
  115.7 8.6 %copy-start.28 = (f32[1,64,128]{2,1,0:T(8,128)}, f32[1,64,128]{2,1,0:T(8,128)S(1)}, u32[]{:S(2)}) copy-start(f32[1,64,128]{2,1,0:T(8,128)S(1)} %collective-permute-done.6) | copy-start | bytes 98308
  119.9 4.4 %copy-start.30 = (f32[1,64,128]{2,1,0:T(8,128)}, f32[1,64,128]{2,1,0:T(8,128)S(1)}, u32[]{:S(2)}) copy-start(f32[1,64,128]{2,1,0:T(8,128)S(1)} %collective-permute-done.7) | copy-start | bytes 98308
  119.9 2.6 collective-permute-start.8
  121.2 3.1 collective-permute-start.9
  131.6 11.6 %collective-permute-start.11 = (f32[34,66,1]{1,2,0:T(1,128)}, f32[34,66,1]{1,2,0:T(1,128)}, u32[]{:S(2)}, u32[]{:S(2)}) collective-permute-start(f32[34,66,1]{1,2,0:T(1,128)} %copy.22), channel_id=1, source_target_pairs={{1,0},{2,1},{3,2},{5,4},{6,5},{7,6},{9,8},{10,9},{11,10},{13,12},{... | collective-permute-start | bytes 26936 | tf_op jit(solution)/shard_map/ppermute | solution.py:19
  132.9 8.1 %collective-permute-start.10 = (f32[34,66,1]{1,2,0:T(1,128)}, f32[34,66,1]{1,2,0:T(1,128)}, u32[]{:S(2)}, u32[]{:S(2)}) collective-permute-start(f32[34,66,1]{1,2,0:T(1,128)} %copy.20), channel_id=1, source_target_pairs={{0,1},{1,2},{2,3},{4,5},{5,6},{6,7},{8,9},{9,10},{10,11},{12,13},{... | collective-permute-start | bytes 26936 | tf_op jit(solution)/shard_map/ppermute | solution.py:17
  145.6 4.2 %copy-start.22 = (f32[32,64,128]{2,1,0:T(8,128)S(1)}, f32[32,64,128]{2,1,0:T(8,128)}, u32[]{:S(2)}) copy-start(f32[32,64,128]{2,1,0:T(8,128)} %get-tuple-element.36) | copy-start | bytes 3145732
  145.7 4.2 %copy-start.29 = (f32[1,64,128]{2,1,0:T(8,128)S(1)}, f32[1,64,128]{2,1,0:T(8,128)}, u32[]{:S(2)}) copy-start(f32[1,64,128]{2,1,0:T(8,128)} %copy-done.28) | copy-start | bytes 98308
  149.8 9.8 %copy-start.17 = (f32[32,64,128]{2,1,0:T(8,128)S(1)}, f32[32,64,128]{2,1,0:T(8,128)}, u32[]{:S(2)}) copy-start(f32[32,64,128]{2,1,0:T(8,128)} %get-tuple-element.33) | copy-start | bytes 3145732
  159.7 9.5 %copy-start.10 = (f32[32,64,128]{2,1,0:T(8,128)}, f32[32,64,128]{2,1,0:T(8,128)S(1)}, u32[]{:S(2)}) copy-start(f32[32,64,128]{2,1,0:T(8,128)S(1)} %get-tuple-element.31) | copy-start | bytes 3145732
  159.8 8.7 %copy-start.6 = (f32[32,64,128]{2,1,0:T(8,128)}, f32[32,64,128]{2,1,0:T(8,128)S(1)}, u32[]{:S(2)}) copy-start(f32[32,64,128]{2,1,0:T(8,128)S(1)} %div.32) | copy-start | bytes 3145732
  159.9 4.4 %collective-permute-start.12 = (f32[1,64,128]{2,1,0:T(8,128)S(1)}, f32[1,64,128]{2,1,0:T(8,128)S(1)}, u32[]{:S(2)}, u32[]{:S(2)}) collective-permute-start(f32[1,64,128]{2,1,0:T(8,128)S(1)} %get-tuple-element.78), channel_id=1, source_target_pairs={{0,8},{8,16},{16,24},{1,9},{9,17},{17,25},{2,10},{10,18},{18,26},{... | collective-permute-start | bytes 98312 | tf_op jit(solution)/shard_map/ppermute | solution.py:17
  162.7 5.8 %collective-permute-start.13 = (f32[1,64,128]{2,1,0:T(8,128)S(1)}, f32[1,64,128]{2,1,0:T(8,128)S(1)}, u32[]{:S(2)}, u32[]{:S(2)}) collective-permute-start(f32[1,64,128]{2,1,0:T(8,128)S(1)} %get-tuple-element.79), channel_id=1, source_target_pairs={{8,0},{16,8},{24,16},{9,1},{17,9},{25,17},{10,2},{18,10},{26,18},{... | collective-permute-start | bytes 98312 | tf_op jit(solution)/shard_map/ppermute | solution.py:19
  164.3 4.9 %copy-start.24 = (f32[1,64,128]{2,1,0:T(8,128)}, f32[1,64,128]{2,1,0:T(8,128)S(1)}, u32[]{:S(2)}) copy-start(f32[1,64,128]{2,1,0:T(8,128)S(1)} %collective-permute-done.12) | copy-start | bytes 98308
  169.1 33.1 %collective-permute-start.14 = (f32[34,1,128]{2,1,0:T(1,128)}, f32[34,1,128]{2,1,0:T(1,128)}, u32[]{:S(2)}, u32[]{:S(2)}) collective-permute-start(f32[34,1,128]{2,1,0:T(1,128)} %get-tuple-element.70), channel_id=1, source_target_pairs={{0,4},{1,5},{2,6},{3,7},{8,12},{9,13},{10,14},{11,15},{16,20},{17,... | collective-permute-start | bytes 52232 | tf_op jit(solution)/shard_map/ppermute | solution.py:17
  171.0 31.2 %collective-permute-start.15 = (f32[34,1,128]{2,1,0:T(1,128)}, f32[34,1,128]{2,1,0:T(1,128)}, u32[]{:S(2)}, u32[]{:S(2)}) collective-permute-start(f32[34,1,128]{2,1,0:T(1,128)} %get-tuple-element.71), channel_id=1, source_target_pairs={{4,0},{5,1},{6,2},{7,3},{12,8},{13,9},{14,10},{15,11},{20,16},{21,... | collective-permute-start | bytes 52232 | tf_op jit(solution)/shard_map/ppermute | solution.py:19
  210.2 12.0 %collective-permute-start.17 = (f32[34,66,1]{1,2,0:T(1,128)}, f32[34,66,1]{1,2,0:T(1,128)}, u32[]{:S(2)}, u32[]{:S(2)}) collective-permute-start(f32[34,66,1]{1,2,0:T(1,128)} %copy.26), channel_id=1, source_target_pairs={{1,0},{2,1},{3,2},{5,4},{6,5},{7,6},{9,8},{10,9},{11,10},{13,12},{... | collective-permute-start | bytes 26936 | tf_op jit(solution)/shard_map/ppermute | solution.py:19
  211.5 8.4 %collective-permute-start.16 = (f32[34,66,1]{1,2,0:T(1,128)}, f32[34,66,1]{1,2,0:T(1,128)}, u32[]{:S(2)}, u32[]{:S(2)}) collective-permute-start(f32[34,66,1]{1,2,0:T(1,128)} %copy.24), channel_id=1, source_target_pairs={{0,1},{1,2},{2,3},{4,5},{5,6},{6,7},{8,9},{9,10},{10,11},{12,13},{... | collective-permute-start | bytes 26936 | tf_op jit(solution)/shard_map/ppermute | solution.py:17
  224.6 4.2 %copy-start.1 = (f32[34,66,130]{2,1,0:T(8,128)S(1)}, f32[34,66,130]{2,1,0:T(8,128)}, u32[]{:S(2)}) copy-start(f32[34,66,130]{2,1,0:T(8,128)} %get-tuple-element.41) | copy-start | bytes 3500644
  224.6 4.2 %copy-start.4 = (f32[34,66,130]{2,1,0:T(8,128)S(1)}, f32[34,66,130]{2,1,0:T(8,128)}, u32[]{:S(2)}) copy-start(f32[34,66,130]{2,1,0:T(8,128)} %get-tuple-element.42) | copy-start | bytes 3500644
  224.6 4.2 %copy-start.7 = (f32[32,64,128]{2,1,0:T(8,128)S(1)}, f32[32,64,128]{2,1,0:T(8,128)}, u32[]{:S(2)}) copy-start(f32[32,64,128]{2,1,0:T(8,128)} %copy-done.6) | copy-start | bytes 3145732
  224.6 4.5 %copy-start.11 = (f32[32,64,128]{2,1,0:T(8,128)S(1)}, f32[32,64,128]{2,1,0:T(8,128)}, u32[]{:S(2)}) copy-start(f32[32,64,128]{2,1,0:T(8,128)} %copy-done.10) | copy-start | bytes 3145732
  224.6 4.8 %copy-start.18 = (f32[32,64,128]{2,1,0:T(8,128)S(1)}, f32[32,64,128]{2,1,0:T(8,128)}, u32[]{:S(2)}) copy-start(f32[32,64,128]{2,1,0:T(8,128)} %get-tuple-element.33) | copy-start | bytes 3145732
  224.6 4.8 %copy-start.25 = (f32[1,64,128]{2,1,0:T(8,128)S(1)}, f32[1,64,128]{2,1,0:T(8,128)}, u32[]{:S(2)}) copy-start(f32[1,64,128]{2,1,0:T(8,128)} %copy-done.24) | copy-start | bytes 98308
  224.6 4.8 %copy-start.27 = (f32[1,64,128]{2,1,0:T(8,128)S(1)}, f32[1,64,128]{2,1,0:T(8,128)}, u32[]{:S(2)}) copy-start(f32[1,64,128]{2,1,0:T(8,128)} %copy-done.26) | copy-start | bytes 98308
  229.4 15.1 %copy-start.23 = (f32[32,64,128]{2,1,0:T(8,128)S(1)}, f32[32,64,128]{2,1,0:T(8,128)}, u32[]{:S(2)}) copy-start(f32[32,64,128]{2,1,0:T(8,128)} %param.5) | copy-start | bytes 3145732
  239.0 6.8 %copy-start.14 = (f32[32,64,128]{2,1,0:T(8,128)}, f32[32,64,128]{2,1,0:T(8,128)S(1)}, u32[]{:S(2)}) copy-start(f32[32,64,128]{2,1,0:T(8,128)S(1)} %get-tuple-element.29) | copy-start | bytes 3145732
  239.0 6.8 %copy-start.19 = (f32[32,64,128]{2,1,0:T(8,128)}, f32[32,64,128]{2,1,0:T(8,128)S(1)}, u32[]{:S(2)}) copy-start(f32[32,64,128]{2,1,0:T(8,128)S(1)} %get-tuple-element.30) | copy-start | bytes 3145732
  239.7 36.0 %collective-permute-start.18 = (f32[1,64,128]{2,1,0:T(8,128)}, f32[1,64,128]{2,1,0:T(8,128)}, u32[]{:S(2)}, u32[]{:S(2)}) collective-permute-start(f32[1,64,128]{2,1,0:T(8,128)} %get-tuple-element.76), channel_id=1, source_target_pairs={{0,8},{8,16},{16,24},{1,9},{9,17},{17,25},{2,10},{10,18},{18,26},{... | collective-permute-start | bytes 98312 | tf_op jit(solution)/shard_map/ppermute | solution.py:17
  243.2 32.5 %collective-permute-start.19 = (f32[1,64,128]{2,1,0:T(8,128)}, f32[1,64,128]{2,1,0:T(8,128)}, u32[]{:S(2)}, u32[]{:S(2)}) collective-permute-start(f32[1,64,128]{2,1,0:T(8,128)} %get-tuple-element.77), channel_id=1, source_target_pairs={{8,0},{16,8},{24,16},{9,1},{17,9},{25,17},{10,2},{18,10},{26,18},{... | collective-permute-start | bytes 98312 | tf_op jit(solution)/shard_map/ppermute | solution.py:19
  276.7 6.5 %collective-permute-start.20 = (f32[34,1,128]{2,1,0:T(1,128)S(1)}, f32[34,1,128]{2,1,0:T(1,128)S(1)}, u32[]{:S(2)}, u32[]{:S(2)}) collective-permute-start(f32[34,1,128]{2,1,0:T(1,128)S(1)} %get-tuple-element.66), channel_id=1, source_target_pairs={{0,4},{1,5},{2,6},{3,7},{8,12},{9,13},{10,14},{11,15},{16,20},{17,... | collective-permute-start | bytes 52232 | tf_op jit(solution)/shard_map/ppermute | solution.py:17
  278.0 5.2 %copy-start.15 = (f32[32,64,128]{2,1,0:T(8,128)S(1)}, f32[32,64,128]{2,1,0:T(8,128)}, u32[]{:S(2)}) copy-start(f32[32,64,128]{2,1,0:T(8,128)} %copy-done.14) | copy-start | bytes 3145732
  278.1 5.2 %collective-permute-start.21 = (f32[34,1,128]{2,1,0:T(1,128)S(1)}, f32[34,1,128]{2,1,0:T(1,128)S(1)}, u32[]{:S(2)}, u32[]{:S(2)}) collective-permute-start(f32[34,1,128]{2,1,0:T(1,128)S(1)} %get-tuple-element.67), channel_id=1, source_target_pairs={{4,0},{5,1},{6,2},{7,3},{12,8},{13,9},{14,10},{15,11},{20,16},{21,... | collective-permute-start | bytes 52232 | tf_op jit(solution)/shard_map/ppermute | solution.py:19
  290.7 11.9 %collective-permute-start.23 = (f32[34,66,1]{1,2,0:T(1,128)}, f32[34,66,1]{1,2,0:T(1,128)}, u32[]{:S(2)}, u32[]{:S(2)}) collective-permute-start(f32[34,66,1]{1,2,0:T(1,128)} %copy.30), channel_id=1, source_target_pairs={{1,0},{2,1},{3,2},{5,4},{6,5},{7,6},{9,8},{10,9},{11,10},{13,12},{... | collective-permute-start | bytes 26936 | tf_op jit(solution)/shard_map/ppermute | solution.py:19
  292.0 8.4 %collective-permute-start.22 = (f32[34,66,1]{1,2,0:T(1,128)}, f32[34,66,1]{1,2,0:T(1,128)}, u32[]{:S(2)}, u32[]{:S(2)}) collective-permute-start(f32[34,66,1]{1,2,0:T(1,128)} %copy.28), channel_id=1, source_target_pairs={{0,1},{1,2},{2,3},{4,5},{5,6},{6,7},{8,9},{9,10},{10,11},{12,13},{... | collective-permute-start | bytes 26936 | tf_op jit(solution)/shard_map/ppermute | solution.py:17
  305.0 4.2 %copy-start.8 = (f32[32,64,128]{2,1,0:T(8,128)S(1)}, f32[32,64,128]{2,1,0:T(8,128)}, u32[]{:S(2)}) copy-start(f32[32,64,128]{2,1,0:T(8,128)} %copy-done.6) | copy-start | bytes 3145732
  305.0 4.5 %copy-start.12 = (f32[32,64,128]{2,1,0:T(8,128)S(1)}, f32[32,64,128]{2,1,0:T(8,128)}, u32[]{:S(2)}) copy-start(f32[32,64,128]{2,1,0:T(8,128)} %copy-done.10) | copy-start | bytes 3145732
  305.0 4.8 %copy-start.16 = (f32[32,64,128]{2,1,0:T(8,128)S(1)}, f32[32,64,128]{2,1,0:T(8,128)}, u32[]{:S(2)}) copy-start(f32[32,64,128]{2,1,0:T(8,128)} %copy-done.14) | copy-start | bytes 3145732
  (12 other events, 38.2 us)
